TPU v7x, 256 devices: a whole 4x4x8 slice. The times are simulated.
256 devices in a mesh: aa: 32 (over y, z_hi, x), ba: 2 (over core), col: 4 (over z_lo).
Axes of the slice: x: 4, y: 4, z: 8 (z_hi: 2, z_lo: 4; z = z_hi * 4 + z_lo), core: 2. Of those that a mesh axis runs over, the one named last changes fastest.
Arguments:
- tokens: bfloat16 [8192, 7168], P('aa', ('ba', 'col')), may hold values from -6 to 6
- expert_ids: int32 [8192, 8], P('aa'), may hold values from 0 to 383, as said below
- route_weight: float32 [8192, 8], P('aa'), may hold values from 0.5 to 2
- w_gate: bfloat16 [32, 7168, 2048], P('aa', None, ('ba', 'col')), may hold values from -0.0625 to 0.0625
- w_up: bfloat16 [32, 7168, 2048], P('aa', None, ('ba', 'col')), may hold values from -0.0625 to 0.0625
- w_down: bfloat16 [32, 2048, 7168], P('aa', ('ba', 'col')), may hold values from -0.125 to 0.125
Outputs:
- mixed: bfloat16 [8192, 7168], P('aa', ('ba', 'col'))
Inputs may be any that keep to these rules, and one draw needn't show every extreme that they name: `expert_ids`: each row names 8 different experts.
All inputs are finite; a program needn't handle non-finite values.
Results may differ from a plain program's by a relative error of at most 0.015.
Values may be sent and summed in bfloat16 or wider, within the bound.
No kernel may reach another device: no remote copies, remote signals or barrier semaphores. Data moves between devices by JAX's collectives and lax.ppermute only.
A program may use at most 64 MiB of HBM per device.

v0:
```python
import jax
import jax.numpy as jnp
from jax import lax
from jax.sharding import PartitionSpec as P

CAP = 8


def gathered_by_axis(shard, axes, dim):
    for axis in reversed(axes):
        shard = lax.all_gather(shard, axis, axis=dim, tiled=True)
    return shard


def split_up(shard, dim, peers):
    before, after = (shard.shape[:dim], shard.shape[dim + 1 :])
    return jnp.moveaxis(shard.reshape(*before, peers, -1, *after), dim, 0)


def sent_and_summed(shard, axis, dim):
    parts = split_up(shard, dim, lax.axis_size(axis))
    arrived = lax.all_to_all(parts, axis, split_axis=0, concat_axis=0, tiled=True)
    return arrived.astype(jnp.float32).sum(axis=0)


def routing(expert_ids, route_weight, flight, capacity):
    expert_pool = jnp.arange(flight, dtype=jnp.int32)
    matched = expert_ids[:, :, None] == expert_pool[None, None, :]
    counted = jnp.sum(matched.astype(jnp.int32), axis=1)
    shares = jnp.sum(jnp.where(matched, route_weight[:, :, None], 0.0), axis=1)
    before = jnp.cumsum(counted, axis=0) - counted
    retained = (counted > 0) & (before < capacity)
    placed = retained[:, :, None] & (
        before[:, :, None] == jnp.arange(capacity, dtype=jnp.int32)[None, None, :]
    )
    return (placed, shares)


def shards(tokens, expert_ids, route_weight, w_gate, w_up, w_down):
    flight = lax.axis_size("aa")
    placed, shares = routing(expert_ids, route_weight, flight, CAP)
    chooser = placed.astype(jnp.bfloat16)
    local_slice = jnp.einsum(
        "tec,tf->ecf", chooser, tokens, preferred_element_type=jnp.float32
    ).astype(jnp.bfloat16)
    gate_matrix = w_gate[0]
    up_matrix = w_up[0]
    down_matrix = w_down[0]
    arrived = lax.all_to_all(local_slice, "aa", split_axis=0, concat_axis=0, tiled=True)
    flat_rows = arrived.reshape(-1, arrived.shape[2])
    portion = gathered_by_axis(flat_rows, ("ba", "col"), 1)
    gate_sum = jnp.dot(portion, gate_matrix, preferred_element_type=jnp.float32)
    up_sum = jnp.dot(portion, up_matrix, preferred_element_type=jnp.float32)
    hidden = (jax.nn.silu(gate_sum) * up_sum).astype(jnp.bfloat16)
    partial_value = jnp.dot(hidden, down_matrix, preferred_element_type=jnp.float32).astype(
        jnp.bfloat16
    )
    shaped = partial_value.reshape(flight, CAP, partial_value.shape[1])
    summands = lax.optimization_barrier(shaped).astype(jnp.float32)
    summed = sent_and_summed(summands.astype(jnp.bfloat16), ("ba", "col"), 2).astype(jnp.bfloat16)
    merged = lax.all_to_all(summed, "aa", split_axis=0, concat_axis=0, tiled=True)
    combine_weight = placed.astype(jnp.float32) * shares[:, :, None]
    weight_high = combine_weight.astype(jnp.bfloat16)
    weight_low = (combine_weight - weight_high.astype(jnp.float32)).astype(jnp.bfloat16)
    mixed = jnp.einsum("tec,ecf->tf", weight_high, merged, preferred_element_type=jnp.float32)
    mixed = mixed + jnp.einsum(
        "tec,ecf->tf", weight_low, merged, preferred_element_type=jnp.float32
    )
    return mixed.astype(jnp.bfloat16)


def solution(mesh):
    in_specs = (
        P("aa", ("ba", "col")),
        P("aa", None),
        P("aa", None),
        P("aa", None, ("ba", "col")),
        P("aa", None, ("ba", "col")),
        P("aa", ("ba", "col"), None),
    )
    out_specs = P("aa", ("ba", "col"))
    return jax.shard_map(shards, mesh=mesh, in_specs=in_specs, out_specs=out_specs, check_vma=False)
```

profile of v0, /device:TPU:1, one launch (start us, length us, event | category | flops | bytes accessed | tf_op | source)
XLA Modules:
  0.0 245.0 jit_solution(12010816975828189192)
XLA Ops:
  6.5 0.0 copy-start
  6.5 0.0 all-gather.3.cloned.1.call-start
  6.5 0.8 convert_reduce_fusion
  7.3 0.6 reduce-window.6
  7.9 0.2 slice_reduce_fusion
  8.2 0.1 compare_and_fusion
  8.3 0.1 fusion.33
  8.4 0.0 copy-done
  8.4 0.3 convolution_convert_fusion.1
  8.7 27.6 %all_to_all.15 = bf16[32,8,896]{2,1,0:T(8,128)(2,1)} all-to-all(bf16[32,8,896]{2,1,0:T(8,128)(2,1)S(1)} %convolution_convert_fusion.1), channel_id=1, replica_groups=mesh['aa'=32,'ba'=2,'col'=4] {'aa'}, dimensions={0} | all-to-all | bytes 917504 | tf_op jit(solution)/shard_map/all_to_all | solution.py:49
  36.3 0.0 all-gather.3.cloned.1.call-update
  36.4 0.0 all-gather.5.cloned.1.call-start
  36.4 46.1 %all-gather.3.cloned.1.call-done = bf16[256,3584]{1,0:T(8,128)(2,1)} async-done(((bf16[256,896]{1,0:T(8,128)(2,1)}), bf16[256,3584]{1,0:T(8,128)(2,1)}) %all-gather.3.cloned.1.call-update) | async-done | bytes 1835024 | tf_op jit(solution)/shard_map/all_gather | solution.py:11
  82.5 0.0 all-gather.5.cloned.1.call-update
  82.5 20.5 %all-gather.5.cloned.1.call-done = bf16[256,7168]{1,0:T(8,128)(2,1)} async-done(((bf16[256,3584]{1,0:T(8,128)(2,1)}), bf16[256,7168]{1,0:T(8,128)(2,1)}) %all-gather.5.cloned.1.call-update) | async-done | bytes 3670032 | tf_op jit(solution)/shard_map/all_gather | solution.py:11
  103.0 4.3 %fusion.4 = f32[256,256]{1,0:T(8,128)S(1)} fusion(bf16[256,7168]{1,0:T(8,128)(2,1)} %all-gather.5.cloned.1.call-done, bf16[1,7168,256]{2,1,0:T(8,128)(2,1)} %param.9), kind=kOutput, calls=%fused_computation.6 | convolution fusion | flops 939524096 | bytes 7602176 | tf_op jit(solution)/shard_map/dot_general | solution.py:52
  107.3 10.0 %fusion = bf16[32,8,7168]{2,1,0:T(8,128)(2,1)} fusion(bf16[1,256,7168]{2,1,0:T(8,128)(2,1)} %param.11, bf16[256,7168]{1,0:T(8,128)(2,1)} %all-gather.5.cloned.1.call-done, bf16[1,7168,256]{2,1,0:T(8,128)(2,1)} %param.10, f32[256,256]{1,0:T(8,128)S(1)} %fusion.4), kind=kOutput, calls=%fused_computation.1 | convolution fusion | flops 1881276416 | bytes 14942208 | tf_op jit(solution)/shard_map/dot_general | solution.py:55
  117.3 2.8 %copy.54 = bf16[32,8,8,896]{3,2,1,0:T(8,128)(2,1)S(1)} copy(bf16[32,8,8,896]{3,1,2,0:T(8,128)(2,1)} %bitcast.62) | data formatting | bytes 7340032
  120.1 0.6 copy.35
  120.7 86.7 %all_to_all.16 = bf16[8,32,8,896]{3,2,1,0:T(8,128)(2,1)} all-to-all(bf16[8,32,8,896]{3,2,1,0:T(8,128)(2,1)S(1)} %copy.35), channel_id=1, replica_groups=mesh['aa'=32,'ba'=2,'col'=4] {'ba','col'}, dimensions={0} | all-to-all | bytes 7340032 | tf_op jit(solution)/shard_map/all_to_all | solution.py:22
  207.4 0.0 copy-start.1
  207.4 0.0 copy-start.2
  207.4 3.4 %reduce_sum.32 = bf16[32,8,896]{2,1,0:T(8,128)(2,1)} reduce(bf16[8,32,8,896]{3,2,1,0:T(8,128)(2,1)} %all_to_all.16, bf16[]{:T(256)} %constant.15.clone.1), dimensions={0}, to_apply=%region_4.5 | reduce | flops 1605632 | bytes 4128770 | tf_op jit(solution)/shard_map/reduce_sum | solution.py:23
  210.9 10.5 %all-to-all-start.2 = ((bf16[32,8,896]{2,1,0:T(8,128)(2,1)}), bf16[32,8,896]{2,1,0:T(8,128)(2,1)S(1)}, u32[]{:S(2)}, u32[]{:S(2)}) async-start(bf16[32,8,896]{2,1,0:T(8,128)(2,1)} %reduce_sum.32), calls=%async_computation.2 | async-start | bytes 917504 | tf_op jit(solution)/shard_map/all_to_all | solution.py:61
  221.4 0.0 copy-done.1
  221.4 0.0 copy-done.2
  221.5 15.2 %all-to-all-done.2 = bf16[32,8,896]{2,1,0:T(8,128)(2,1)S(1)} async-done(((bf16[32,8,896]{2,1,0:T(8,128)(2,1)}), bf16[32,8,896]{2,1,0:T(8,128)(2,1)S(1)}, u32[]{:S(2)}, u32[]{:S(2)}) %all-to-all-start.2) | async-done | bytes 458784 | tf_op jit(solution)/shard_map/all_to_all | solution.py:61
  236.6 0.4 convolution_bitcast_fusion
  237.0 1.1 fusion.7
  (5 shorter events, 0.1 us)
Async XLA Ops:
  6.5 1.9 copy-start
  6.5 76.0 %all-gather.3.cloned.1.call-start = ((), (), s32[]{:S(2)}) async-start(), calls=%async_computation.3 | async-start | bytes 2293760 | tf_op jit(solution)/shard_map/all_gather | solution.py:11
  36.4 66.7 %all-gather.5.cloned.1.call-start = ((), (), s32[]{:S(2)}) async-start(), calls=%async_computation.4 | async-start | bytes 5505024 | tf_op jit(solution)/shard_map/all_gather | solution.py:11
  207.4 14.0 %copy-start.1 = (s32[256,8]{0,1:T(8,128)S(1)}, s32[256,8]{0,1:T(8,128)}, u32[]{:S(2)}) copy-start(s32[256,8]{0,1:T(8,128)} %param.7) | copy-start | bytes 24580
  207.4 14.0 %copy-start.2 = (f32[256,8]{0,1:T(8,128)S(1)}, f32[256,8]{0,1:T(8,128)}, u32[]{:S(2)}) copy-start(f32[256,8]{0,1:T(8,128)} %param.8) | copy-start | bytes 24580
  210.9 25.8 %all-to-all-start.2 = ((bf16[32,8,896]{2,1,0:T(8,128)(2,1)}), bf16[32,8,896]{2,1,0:T(8,128)(2,1)S(1)}, u32[]{:S(2)}, u32[]{:S(2)}) async-start(bf16[32,8,896]{2,1,0:T(8,128)(2,1)} %reduce_sum.32), calls=%async_computation.2 | async-start | bytes 917504 | tf_op jit(solution)/shard_map/all_to_all | solution.py:61
Sparse Core Ops, SparseCore 0:
  36.5 45.9 all-gather.2
  84.3 18.6 all-gather.4
where the time goes:
time: 247 us; the launch traced here: 245 us
  blocking collectives  114 us (46%)
  waiting for transfers between devices  81.8 us (33%)
  matrix products  16.1 us (7%)
  between operations  13.5 us (5%)
  starting transfers between devices  10.6 us (4%)
  other arithmetic  5.09 us (2%)
  local copies, waits for them, and re-layouts  3.57 us (1%)
    all_to_all x1, blocking collectives, sent_and_summed(): lax.all_to_all(parts, axis, split_axis=0, concat_axis=0, tiled=True)  86.7 us
    all_gather x2, waiting for transfers between devices, gathered_by_axis(): shard = lax.all_gather(shard, axis, axis=dim, tiled=True)  66.6 us
    all_to_all x1, blocking collectives, shards(): lax.all_to_all(local_slice, 'aa', split_axis=0, concat_axis=0, tiled=True)  27.6 us
    all_to_all x1, waiting for transfers between devices, shards(): lax.all_to_all(summed, 'aa', split_axis=0, concat_axis=0, tiled=True)  15.2 us
    all_to_all x1, starting transfers between devices, shards(): lax.all_to_all(summed, 'aa', split_axis=0, concat_axis=0, tiled=True)  10.5 us
    dot_general x1, matrix products, shards(): jnp.dot(hidden, down_matrix, preferred_element_type=jnp.float32)  10 us
  transfers between devices with their start and end apart: 3, of which 3 were waited for; matrix products, arithmetic and copies ran while one was open for 0% of the time, Pallas kernels for 0%

commit v1 on v0

v1 whole, which is shorter than its diff:
```python
import jax
import jax.numpy as jnp
from jax import lax
from jax.experimental import pallas as pl
from jax.experimental.pallas import tpu as pltpu
from jax.sharding import PartitionSpec as P

CAP = 8
F32 = jnp.float32
BF16 = jnp.bfloat16


def mm(a, b):
    return jnp.dot(a, b, preferred_element_type=F32)


def slots_of(ids, experts):
    top, tokens = ids.shape
    pool = lax.broadcasted_iota(jnp.int32, (experts, tokens), 0)
    hit = jnp.zeros((experts, tokens), F32)
    for k in range(top):
        hit = hit + jnp.where(ids[k : k + 1, :] == pool, 1.0, 0.0)
    earlier = lax.broadcasted_iota(jnp.int32, (tokens, tokens), 0)
    later = lax.broadcasted_iota(jnp.int32, (tokens, tokens), 1)
    before = mm(hit.astype(BF16), jnp.where(earlier < later, 1.0, 0.0).astype(BF16))
    rank = before.astype(jnp.int32)
    kept = (hit > 0.0) & (rank < CAP)
    rank = jnp.where(kept, rank, -1)
    return pool, rank


def placed_of(rank, value):
    experts, tokens = rank.shape
    slot = lax.broadcasted_iota(jnp.int32, (experts, CAP, tokens), 1)
    spread = lax.broadcast_in_dim(rank, (experts, CAP, tokens), (0, 2))
    filled = lax.broadcast_in_dim(value, (experts, CAP, tokens), (0, 2))
    return jnp.where(spread == slot, filled, 0.0).reshape(experts * CAP, tokens)


def dispatch_body(ids_ref, tok_ref, out_ref):
    experts, copies, cap, width = out_ref.shape
    _, rank = slots_of(ids_ref[...], experts)
    chooser = placed_of(rank, jnp.ones(rank.shape, F32)).astype(BF16)
    rows = mm(chooser, tok_ref[...]).astype(BF16).reshape(experts, cap, width)
    for j in range(copies):
        out_ref[:, j] = rows


def weights_body(ids_ref, rw_ref, high_ref, low_ref):
    ids = ids_ref[...]
    rw = rw_ref[...]
    pool, rank = slots_of(ids, high_ref.shape[1] // CAP)
    share = jnp.zeros(pool.shape, F32)
    for k in range(ids.shape[0]):
        share = share + jnp.where(ids[k : k + 1, :] == pool, rw[k : k + 1, :], 0.0)
    weight = placed_of(rank, share).T
    high = weight.astype(BF16)
    high_ref[...] = high
    low_ref[...] = (weight - high.astype(F32)).astype(BF16)


def first_body(b_ref, x_ref, wg_ref, wu_ref, g_ref, u_ref):
    x = x_ref[...].reshape(-1, x_ref.shape[3])

    @pl.when(pl.program_id(0) == 0)
    def _():
        g_ref[...] = jnp.zeros_like(g_ref)
        u_ref[...] = jnp.zeros_like(u_ref)

    g_ref[...] += mm(x, wg_ref[0])
    u_ref[...] += mm(x, wu_ref[0])


def second_body(b_ref, x_ref, wg_ref, wu_ref, g0_ref, u0_ref, wd_ref, h_ref, out_ref, g_ref, u_ref):
    step = pl.program_id(0)
    half = pl.num_programs(0) // 2

    @pl.when(step == 0)
    def _():
        g_ref[...] = g0_ref[...]
        u_ref[...] = u0_ref[...]

    @pl.when(step < half)
    def _():
        x = x_ref[...].reshape(-1, x_ref.shape[3])
        g_ref[...] += mm(x, wg_ref[0])
        u_ref[...] += mm(x, wu_ref[0])

    @pl.when(step == half - 1)
    def _():
        g = g_ref[...]
        h_ref[...] = (g / (1.0 + jnp.exp(-g)) * u_ref[...]).astype(BF16)

    @pl.when(step >= half)
    def _():
        out_ref[...] = mm(h_ref[...], wd_ref[...]).astype(BF16).reshape(out_ref.shape)


def third_body(b_ref, h_ref, wd_ref, r_ref, out_ref):
    own = mm(h_ref[...], wd_ref[...])
    other = r_ref[...].reshape(own.shape).astype(F32)
    out_ref[...] = (own + other).astype(BF16).reshape(out_ref.shape)


def combine_body(r_ref, high_ref, low_ref, out_ref):
    experts, copies, cap, width = r_ref.shape
    total = r_ref[:, 0].astype(F32)
    for j in range(1, copies):
        total = total + r_ref[:, j].astype(F32)
    rows = total.astype(BF16).reshape(experts * cap, width)
    out_ref[...] = (mm(high_ref[...], rows) + mm(low_ref[...], rows)).astype(BF16)


def shards(tokens, expert_ids, route_weight, w_gate, w_up, w_down):
    n_aa, n_ba, n_col = lax.axis_size("aa"), lax.axis_size("ba"), lax.axis_size("col")
    n_tok, width = tokens.shape
    hid = w_gate.shape[2]
    n_slot = n_aa * CAP
    ids = expert_ids.T
    rw = route_weight.T
    b = lax.axis_index("ba").astype(jnp.int32).reshape(1)
    wg = w_gate.reshape(n_ba * n_col, width, hid)
    wu = w_up.reshape(n_ba * n_col, width, hid)
    wd = w_down[0]
    swap = [(i, n_ba - 1 - i) for i in range(n_ba)]
    axes = ("aa", "col")
    big = jax.ShapeDtypeStruct((n_aa, n_col, CAP, width), BF16)
    block = (n_aa, 1, CAP, width)
    acc = jax.ShapeDtypeStruct((n_slot, hid), F32)
    whole = lambda shape: pl.BlockSpec(shape, lambda i, b: (0,) * len(shape))

    picked = pl.pallas_call(dispatch_body, out_shape=big, name="dispatch")(ids, tokens)
    mine = lax.all_to_all(picked.reshape(n_aa * n_col, CAP, width), axes, 0, 0, tiled=True)
    mine = mine.reshape(big.shape)
    theirs = lax.ppermute(mine, "ba", swap)

    g, u = pl.pallas_call(
        first_body,
        name="first",
        grid_spec=pltpu.PrefetchScalarGridSpec(
            num_scalar_prefetch=1,
            grid=(n_col,),
            in_specs=[
                pl.BlockSpec(block, lambda i, b: (0, i, 0, 0)),
                pl.BlockSpec((1, width, hid), lambda i, b: (b[0] * n_col + i, 0, 0)),
                pl.BlockSpec((1, width, hid), lambda i, b: (b[0] * n_col + i, 0, 0)),
            ],
            out_specs=[whole((n_slot, hid)), whole((n_slot, hid))],
        ),
        out_shape=[acc, acc],
    )(b, mine, wg, wu)

    last = n_col - 1
    w_at = lambda i, b: ((1 - b[0]) * n_col + jnp.minimum(i, last), 0, 0)
    hidden, sent = pl.pallas_call(
        second_body,
        name="second",
        grid_spec=pltpu.PrefetchScalarGridSpec(
            num_scalar_prefetch=1,
            grid=(2 * n_col,),
            in_specs=[
                pl.BlockSpec(block, lambda i, b: (0, jnp.minimum(i, last), 0, 0)),
                pl.BlockSpec((1, width, hid), w_at),
                pl.BlockSpec((1, width, hid), w_at),
                whole((n_slot, hid)),
                whole((n_slot, hid)),
                pl.BlockSpec((hid, width), lambda i, b: (0, (1 - b[0]) * n_col + jnp.maximum(i - n_col, 0))),
            ],
            out_specs=[
                whole((n_slot, hid)),
                pl.BlockSpec(block, lambda i, b: (0, jnp.maximum(i - n_col, 0), 0, 0)),
            ],
            scratch_shapes=[pltpu.VMEM((n_slot, hid), F32), pltpu.VMEM((n_slot, hid), F32)],
        ),
        out_shape=[jax.ShapeDtypeStruct((n_slot, hid), BF16), big],
    )(b, theirs, wg, wu, g, u, wd)

    got = lax.ppermute(sent, "ba", swap)
    pair = pl.pallas_call(
        third_body,
        name="third",
        grid_spec=pltpu.PrefetchScalarGridSpec(
            num_scalar_prefetch=1,
            grid=(n_col,),
            in_specs=[
                whole((n_slot, hid)),
                pl.BlockSpec((hid, width), lambda i, b: (0, b[0] * n_col + i)),
                pl.BlockSpec(block, lambda i, b: (0, i, 0, 0)),
            ],
            out_specs=pl.BlockSpec(block, lambda i, b: (0, i, 0, 0)),
        ),
        out_shape=big,
    )(b, hidden, wd, got)

    back = lax.all_to_all(pair.reshape(n_aa * n_col, CAP, width), axes, 0, 0, tiled=True)
    flat = jax.ShapeDtypeStruct((n_tok, n_slot), BF16)
    high, low = pl.pallas_call(weights_body, out_shape=[flat, flat], name="weights")(ids, rw)
    return pl.pallas_call(
        combine_body, out_shape=jax.ShapeDtypeStruct((n_tok, width), BF16), name="combine"
    )(back.reshape(big.shape), high, low)


def solution(mesh):
    in_specs = (
        P("aa", ("ba", "col")),
        P("aa", None),
        P("aa", None),
        P("aa", None, ("ba", "col")),
        P("aa", None, ("ba", "col")),
        P("aa", ("ba", "col"), None),
    )
    out_specs = P("aa", ("ba", "col"))
    return jax.shard_map(shards, mesh=mesh, in_specs=in_specs, out_specs=out_specs, check_vma=False)
```

time: 247 us -> 151 us (0.61)
  blocking collectives: 114 us -> 63.1 us
  waiting for transfers between devices: 81.8 us -> 49.3 us
  Pallas kernels: 0 us -> 25.5 us
  matrix products: 16.1 us -> 0 us
  between operations: 13.5 us -> 0.02 us
  other arithmetic: 5.09 us -> 0 us
    all_gather x2 -> x0, waiting for transfers between devices: 66.6 us -> none  [gathered_by_axis(): shard = lax.all_gather(shard, axis, axis=dim, tiled=True)]
    all_to_all x2 -> x1, blocking collectives: 114 us -> 63.1 us  [shards(): lax.all_to_all(picked.reshape(n_aa * n_col, CAP, width), axes, 0, 0, tile...]
    all_to_all x1, waiting for transfers between devices: 15.2 us -> 45.7 us  [shards(): lax.all_to_all(pair.reshape(n_aa * n_col, CAP, width), axes, 0, 0, tiled=...]
    pallas_call x0 -> x6, Pallas kernels: none -> 25.5 us  [the longest x1 8.49 us: shards(): pl.pallas_call(second_body, name='second', grid_spec=pltpu.PrefetchScalar...]
    dot_general x5 -> x0, matrix products: 16.1 us -> none  [the longest x1 10 us: shards(): jnp.dot(hidden, down_matrix, preferred_element_type=jnp.float32)]
    all_to_all x1, starting transfers between devices: 10.5 us -> 6.2 us  [shards(): lax.all_to_all(pair.reshape(n_aa * n_col, CAP, width), axes, 0, 0, tiled=...]
    reduce_sum x3 -> x0, other arithmetic: 4.25 us -> none  [the longest x1 3.43 us: sent_and_summed(): return arrived.astype(jnp.float32).sum(axis=0)]
    ppermute x0 -> x2, starting transfers between devices: none -> 3.89 us  [the longest x1 2.66 us: shards(): theirs = lax.ppermute(mine, 'ba', swap)]
  transfers between devices with their start and end apart: 3 -> 3, of which waited for: 3 -> 2; matrix products, arithmetic and copies ran while one was open for 0% -> 0% of each run, Pallas kernels for 0% -> 4%
where the time goes in v1:
time: 151 us
  blocking collectives  63.1 us (42%)
  waiting for transfers between devices  49.3 us (33%)
  Pallas kernels  25.5 us (17%)
  starting transfers between devices  10.1 us (7%)
  local copies, waits for them, and re-layouts  2.48 us (2%)
    all_to_all x1, blocking collectives, shards(): lax.all_to_all(picked.reshape(n_aa * n_col, CAP, width), axes, 0, 0, tile...  63.1 us
    all_to_all x1, waiting for transfers between devices, shards(): lax.all_to_all(pair.reshape(n_aa * n_col, CAP, width), axes, 0, 0, tiled=...  45.7 us
    pallas_call x1, Pallas kernels, shards(): pl.pallas_call(second_body, name='second', grid_spec=pltpu.PrefetchScalar...  8.49 us
    all_to_all x1, starting transfers between devices, shards(): lax.all_to_all(pair.reshape(n_aa * n_col, CAP, width), axes, 0, 0, tiled=...  6.2 us
    pallas_call x1, Pallas kernels, shards(): pl.pallas_call(first_body, name='first', grid_spec=pltpu.PrefetchScalarGr...  4.96 us
    pallas_call x1, Pallas kernels, shards(): pl.pallas_call(third_body, name='third', grid_spec=pltpu.PrefetchScalarGr...  4.64 us
    ppermute x1, waiting for transfers between devices, shards(): got = lax.ppermute(sent, 'ba', swap)  3.62 us
  transfers between devices with their start and end apart: 3, of which 2 were waited for; matrix products, arithmetic and copies ran while one was open for 0% of the time, Pallas kernels for 4%

profile of v1, /device:TPU:1, one launch (start us, length us, event | category | flops | bytes accessed | tf_op | source)
XLA Modules:
  0.0 150.5 jit_solution(14919472924684812868)
XLA Ops:
  0.0 2.7 %dispatch.1 = bf16[32,4,8,896]{3,2,1,0:T(8,128)(2,1)} custom-call(s32[8,256]{1,0:T(8,128)} %bitcast.21, bf16[256,896]{1,0:T(8,128)(2,1)} %tok_ref.1), custom_call_target="tpu_custom_call" | custom-call | tf_op jit(solution)/shard_map/dispatch/pallas_call | solution.py:132
  2.7 63.1 %all_to_all.10 = bf16[128,8,896]{2,1,0:T(8,128)(2,1)S(1)} all-to-all(bf16[128,8,896]{2,1,0:T(8,128)(2,1)} %bitcast.19), channel_id=1, replica_groups=mesh['aa'=32,'ba'=2,'col'=4] {'aa','col'}, dimensions={0} | all-to-all | bytes 3670016 | tf_op jit(solution)/shard_map/all_to_all | solution.py:133
  65.9 0.0 copy-start
  65.9 2.7 %collective-permute-start = (bf16[32,4,8,896]{3,2,1,0:T(8,128)(2,1)S(1)}, bf16[32,4,8,896]{3,2,1,0:T(8,128)(2,1)}, u32[]{:S(2)}, u32[]{:S(2)}) collective-permute-start(bf16[32,4,8,896]{3,2,1,0:T(8,128)(2,1)S(1)} %bitcast.16), channel_id=1, source_target_pairs={{0,4},{4,0},{1,5},{5,1},{2,6},{6,2},{3,7},{7,3},{8,12},{12,8},{9,1... | collective-permute-start | bytes 5505032 | tf_op jit(solution)/shard_map/ppermute | solution.py:135
  68.5 0.0 copy-done
  68.5 5.0 %first.1 = (f32[256,256]{1,0:T(8,128)}, f32[256,256]{1,0:T(8,128)}) custom-call(s32[1]{0:T(128)} %bitcast.b_ref, bf16[32,4,8,896]{3,2,1,0:T(8,128)(2,1)} %bitcast.17, bf16[8,896,256]{2,1,0:T(8,128)(2,1)} %bitcast.10, bf16[8,896,256]{2,1,0:T(8,128)(2,1)} %bitcast.12), custom_call_target="tpu_custom_call" | custom-call | tf_op jit(solution)/shard_map/first/pallas_call | solution.py:137
  73.5 0.0 collective-permute-done.x_ref
  73.5 8.5 %second.1 = (bf16[256,256]{1,0:T(8,128)(2,1)}, bf16[32,4,8,896]{3,2,1,0:T(8,128)(2,1)}) custom-call(s32[1]{0:T(128)} %bitcast.b_ref, bf16[32,4,8,896]{3,2,1,0:T(8,128)(2,1)} %collective-permute-done.x_ref, bf16[8,896,256]{2,1,0:T(8,128)(2,1)} %bitcast.11, bf16[8,896,256]{2,1,0:T(8,128)(2,1)} %bitcast.13, f32[256,256]{1,0:T(8,128)} %get-tuple-element.11.g0_ref, ...), custom_call_target="tpu_custom_call" | custom-call | tf_op jit(solution)/shard_map/second/pallas_call | solution.py:155
  82.0 1.2 collective-permute-start.1
  83.2 3.6 %collective-permute-done.1.r_ref = bf16[32,4,8,896]{3,2,1,0:T(8,128)(2,1)S(1)} collective-permute-done((bf16[32,4,8,896]{3,2,1,0:T(8,128)(2,1)}, bf16[32,4,8,896]{3,2,1,0:T(8,128)(2,1)S(1)}, u32[]{:S(2)}, u32[]{:S(2)}) %collective-permute-start.1) | collective-permute-done | bytes 1835040 | tf_op jit(solution)/shard_map/ppermute | solution.py:178
  86.8 0.0 copy-start.2
  86.9 1.2 copy-done.2
  88.1 4.6 %third.1 = bf16[32,4,8,896]{3,2,1,0:T(8,128)(2,1)} custom-call(s32[1]{0:T(128)} %bitcast.b_ref, bf16[256,256]{1,0:T(8,128)(2,1)} %get-tuple-element.13.h_ref, bf16[256,7168]{1,0:T(8,128)(2,1)} %bitcast.15, bf16[32,4,8,896]{3,2,1,0:T(8,128)(2,1)} %copy-done.2), custom_call_target="tpu_custom_call" | custom-call | tf_op jit(solution)/shard_map/third/pallas_call | solution.py:179
  92.7 6.2 %all-to-all-start.1 = ((bf16[128,8,896]{2,1,0:T(8,128)(2,1)}), bf16[128,8,896]{2,1,0:T(8,128)(2,1)S(1)}, u32[]{:S(2)}, u32[]{:S(2)}) async-start(bf16[128,8,896]{2,1,0:T(8,128)(2,1)} %bitcast.20), calls=%async_computation.1 | async-start | bytes 3670016 | tf_op jit(solution)/shard_map/all_to_all | solution.py:195
  98.9 1.7 %weights.1 = (bf16[256,256]{1,0:T(8,128)(2,1)}, bf16[256,256]{1,0:T(8,128)(2,1)}) custom-call(s32[8,256]{1,0:T(8,128)} %bitcast.22, f32[8,256]{1,0:T(8,128)} %bitcast.23), custom_call_target="tpu_custom_call" | custom-call | tf_op jit(solution)/shard_map/weights/pallas_call | solution.py:197
  100.7 45.7 %all-to-all-done.1 = bf16[128,8,896]{2,1,0:T(8,128)(2,1)S(1)} async-done(((bf16[128,8,896]{2,1,0:T(8,128)(2,1)}), bf16[128,8,896]{2,1,0:T(8,128)(2,1)S(1)}, u32[]{:S(2)}, u32[]{:S(2)}) %all-to-all-start.1) | async-done | bytes 1835040 | tf_op jit(solution)/shard_map/all_to_all | solution.py:195
  146.4 0.0 copy-start.1
  146.4 1.2 copy-done.1
  147.6 2.9 %combine.1 = bf16[256,896]{1,0:T(8,128)(2,1)} custom-call(bf16[32,4,8,896]{3,2,1,0:T(8,128)(2,1)} %bitcast.18, bf16[256,256]{1,0:T(8,128)(2,1)} %get-tuple-element.15.high_ref, bf16[256,256]{1,0:T(8,128)(2,1)} %get-tuple-element.16.low_ref), custom_call_target="tpu_custom_call" | custom-call | tf_op jit(solution)/shard_map/combine/pallas_call | solution.py:198
Async XLA Ops:
  65.9 2.7 %copy-start = (bf16[128,8,896]{2,1,0:T(8,128)(2,1)}, bf16[128,8,896]{2,1,0:T(8,128)(2,1)S(1)}, u32[]{:S(2)}) copy-start(bf16[128,8,896]{2,1,0:T(8,128)(2,1)S(1)} %all_to_all.10) | copy-start | bytes 5505028
  65.9 7.6 %collective-permute-start = (bf16[32,4,8,896]{3,2,1,0:T(8,128)(2,1)S(1)}, bf16[32,4,8,896]{3,2,1,0:T(8,128)(2,1)}, u32[]{:S(2)}, u32[]{:S(2)}) collective-permute-start(bf16[32,4,8,896]{3,2,1,0:T(8,128)(2,1)S(1)} %bitcast.16), channel_id=1, source_target_pairs={{0,4},{4,0},{1,5},{5,1},{2,6},{6,2},{3,7},{7,3},{8,12},{12,8},{9,1... | collective-permute-start | bytes 5505032 | tf_op jit(solution)/shard_map/ppermute | solution.py:135
  82.0 4.9 %collective-permute-start.1 = (bf16[32,4,8,896]{3,2,1,0:T(8,128)(2,1)}, bf16[32,4,8,896]{3,2,1,0:T(8,128)(2,1)S(1)}, u32[]{:S(2)}, u32[]{:S(2)}) collective-permute-start(bf16[32,4,8,896]{3,2,1,0:T(8,128)(2,1)} %get-tuple-element.14), channel_id=1, source_target_pairs={{0,4},{4,0},{1,5},{5,1},{2,6},{6,2},{3,7},{7,3},{8,12},{12,8},{9,1... | collective-permute-start | bytes 5505032 | tf_op jit(solution)/shard_map/ppermute | solution.py:178
  86.8 1.2 copy-start.2
  92.7 53.6 %all-to-all-start.1 = ((bf16[128,8,896]{2,1,0:T(8,128)(2,1)}), bf16[128,8,896]{2,1,0:T(8,128)(2,1)S(1)}, u32[]{:S(2)}, u32[]{:S(2)}) async-start(bf16[128,8,896]{2,1,0:T(8,128)(2,1)} %bitcast.20), calls=%async_computation.1 | async-start | bytes 3670016 | tf_op jit(solution)/shard_map/all_to_all | solution.py:195
  146.4 1.2 copy-start.1

commit v2 on v1

v2 whole, which is shorter than its diff:
```python
import jax
import jax.numpy as jnp
from jax import lax
from jax.experimental import pallas as pl
from jax.experimental.pallas import tpu as pltpu
from jax.sharding import PartitionSpec as P

CAP = 8
F32 = jnp.float32
BF16 = jnp.bfloat16


def held(x):
    return pltpu.with_memory_space_constraint(x, pltpu.VMEM)


def limit(mib):
    return pltpu.CompilerParams(vmem_limit_bytes=mib * 2**20)


def mm(a, b):
    return jnp.dot(a, b, preferred_element_type=F32)


def slots_of(ids, experts):
    top, tokens = ids.shape
    pool = lax.broadcasted_iota(jnp.int32, (experts, tokens), 0)
    hit = jnp.zeros((experts, tokens), F32)
    for k in range(top):
        hit = hit + jnp.where(ids[k : k + 1, :] == pool, 1.0, 0.0)
    earlier = lax.broadcasted_iota(jnp.int32, (tokens, tokens), 0)
    later = lax.broadcasted_iota(jnp.int32, (tokens, tokens), 1)
    before = mm(hit.astype(BF16), jnp.where(earlier < later, 1.0, 0.0).astype(BF16))
    rank = before.astype(jnp.int32)
    kept = (hit > 0.0) & (rank < CAP)
    rank = jnp.where(kept, rank, -1)
    return pool, rank


def placed_of(rank, value):
    experts, tokens = rank.shape
    slot = lax.broadcasted_iota(jnp.int32, (experts, CAP, tokens), 1)
    spread = lax.broadcast_in_dim(rank, (experts, CAP, tokens), (0, 2))
    filled = lax.broadcast_in_dim(value, (experts, CAP, tokens), (0, 2))
    return jnp.where(spread == slot, filled, 0.0).reshape(experts * CAP, tokens)


def prepare_body(ids_ref, rw_ref, tok_ref, out_ref, high_ref, low_ref):
    experts, copies, cap, width = out_ref.shape
    ids = ids_ref[...]
    rw = rw_ref[...]
    pool, rank = slots_of(ids, experts)
    chooser = placed_of(rank, jnp.ones(rank.shape, F32)).astype(BF16)
    rows = mm(chooser, tok_ref[...]).astype(BF16).reshape(experts, cap, width)
    for j in range(copies):
        out_ref[:, j] = rows
    share = jnp.zeros(pool.shape, F32)
    for k in range(ids.shape[0]):
        share = share + jnp.where(ids[k : k + 1, :] == pool, rw[k : k + 1, :], 0.0)
    weight = placed_of(rank, share).T
    high = weight.astype(BF16)
    high_ref[...] = high
    low_ref[...] = (weight - high.astype(F32)).astype(BF16)


def gate_up(x_ref, wg_ref, wu_ref, ready):
    copies, width = x_ref.shape[1], x_ref.shape[3]
    g = u = None
    for j in range(copies):
        ready(j)
        x = x_ref[:, j].reshape(-1, width)
        dg = mm(x, wg_ref[j])
        du = mm(x, wu_ref[j])
        g = dg if g is None else g + dg
        u = du if u is None else u + du
    return g, u


def first_body(b_ref, x_ref, wg_hbm, wu_hbm, wd_hbm, g_ref, u_ref, wg_ref, wu_ref, wd_ref, wg0_ref, wu0_ref, sems, late):
    b = b_ref[0]
    copies = x_ref.shape[1]
    near = [
        (
            pltpu.make_async_copy(wg_hbm.at[b * copies + j], wg0_ref.at[j], sems.at[j]),
            pltpu.make_async_copy(wu_hbm.at[b * copies + j], wu0_ref.at[j], sems.at[copies + j]),
        )
        for j in range(copies)
    ]
    far = [
        pltpu.make_async_copy(wg_hbm.at[pl.ds((1 - b) * copies, copies)], wg_ref, late.at[0]),
        pltpu.make_async_copy(wu_hbm.at[pl.ds((1 - b) * copies, copies)], wu_ref, late.at[1]),
        pltpu.make_async_copy(wd_hbm, wd_ref, late.at[2]),
    ]
    for pair in near:
        for move in pair:
            move.start()
    for move in far:
        move.start()

    def ready(j):
        for move in near[j]:
            move.wait()

    g_ref[...], u_ref[...] = gate_up(x_ref, wg0_ref, wu0_ref, ready)
    for move in far:
        move.wait()


def down(b, j, h, wd_ref, copies, width):
    at = pl.multiple_of((b * copies + j) * width, 128)
    return mm(h, wd_ref[:, pl.ds(at, width)])


def second_body(b_ref, x_ref, wg_ref, wu_ref, g_ref, u_ref, wd_ref, h_ref, out_ref):
    experts, copies, cap, width = x_ref.shape
    g, u = gate_up(x_ref, wg_ref, wu_ref, lambda j: None)
    g = g + g_ref[...]
    u = u + u_ref[...]
    h = (g / (1.0 + jnp.exp(-g)) * u).astype(BF16)
    h_ref[...] = h
    for j in range(copies):
        out_ref[:, j] = down(1 - b_ref[0], j, h, wd_ref, copies, width).astype(BF16).reshape(experts, cap, width)


def third_body(b_ref, h_ref, wd_ref, out_ref):
    experts, copies, cap, width = out_ref.shape
    h = h_ref[...]
    for j in range(copies):
        out_ref[:, j] = down(b_ref[0], j, h, wd_ref, copies, width).reshape(experts, cap, width)


def pair_body(own_ref, other_ref, out_ref):
    for j in range(out_ref.shape[1]):
        out_ref[:, j] = (own_ref[:, j] + other_ref[:, j].astype(F32)).astype(BF16)


def combine_body(r_ref, high_ref, low_ref, out_ref):
    experts, copies, cap, width = r_ref.shape
    total = r_ref[:, 0].astype(F32)
    for j in range(1, copies):
        total = total + r_ref[:, j].astype(F32)
    rows = total.astype(BF16).reshape(experts * cap, width)
    out_ref[...] = (mm(high_ref[...], rows) + mm(low_ref[...], rows)).astype(BF16)


def shards(tokens, expert_ids, route_weight, w_gate, w_up, w_down):
    n_aa, n_ba, n_col = lax.axis_size("aa"), lax.axis_size("ba"), lax.axis_size("col")
    n_tok, width = tokens.shape
    hid = w_gate.shape[2]
    n_slot = n_aa * CAP
    ids = expert_ids.T
    rw = route_weight.T
    b = lax.axis_index("ba").astype(jnp.int32).reshape(1)
    params = [w_gate.reshape(n_ba * n_col, width, hid), w_up.reshape(n_ba * n_col, width, hid), w_down[0]]
    swap = [(i, n_ba - 1 - i) for i in range(n_ba)]
    axes = ("aa", "col")
    shape = (n_aa, n_col, CAP, width)
    acc = pltpu.VMEM((n_slot, hid), F32)
    smem = pl.BlockSpec(memory_space=pltpu.SMEM)
    vmem = pl.BlockSpec(memory_space=pltpu.VMEM)

    hbm = pl.BlockSpec(memory_space=pl.ANY)
    flat = pltpu.VMEM((n_tok, n_slot), BF16)
    picked, high, low = pl.pallas_call(
        prepare_body,
        name="prepare",
        in_specs=[vmem] * 3,
        out_shape=[pltpu.VMEM(shape, BF16), flat, flat],
        out_specs=[vmem] * 3,
        compiler_params=limit(8),
    )(ids, rw, tokens)
    mine = lax.all_to_all(picked.reshape(n_aa * n_col, CAP, width), axes, 0, 0, tiled=True)
    mine = mine.reshape(shape)
    theirs = lax.ppermute(mine, "ba", swap)

    part = pltpu.VMEM((n_col, width, hid), BF16)
    g, u, wg, wu, wd = pl.pallas_call(
        first_body,
        name="first",
        in_specs=[smem, vmem] + [hbm] * 3,
        out_shape=[acc, acc, part, part, pltpu.VMEM(params[2].shape, BF16)],
        out_specs=[vmem] * 5,
        scratch_shapes=[part, part, pltpu.SemaphoreType.DMA((2 * n_col,)), pltpu.SemaphoreType.DMA((3,))],
        compiler_params=limit(16),
    )(b, held(mine), *[pltpu.with_memory_space_constraint(p, pltpu.HBM) for p in params])
    wg, wu, wd = held(wg), held(wu), held(wd)

    hidden, sent = pl.pallas_call(
        second_body,
        name="second",
        in_specs=[smem] + [vmem] * 6,
        out_shape=[pltpu.VMEM((n_slot, hid), BF16), pltpu.VMEM(shape, BF16)],
        compiler_params=limit(8),
    )(b, held(theirs), wg, wu, held(g), held(u), wd)

    got = lax.ppermute(sent, "ba", swap)
    own = pl.pallas_call(
        third_body,
        name="third",
        in_specs=[smem] + [vmem] * 2,
        out_shape=pltpu.VMEM(shape, F32),
        compiler_params=limit(8),
    )(b, held(hidden), wd)
    pair = pl.pallas_call(
        pair_body, name="pair", out_shape=pltpu.VMEM(shape, BF16), compiler_params=limit(8)
    )(held(own), held(got))

    back = lax.all_to_all(pair.reshape(n_aa * n_col, CAP, width), axes, 0, 0, tiled=True)
    return pl.pallas_call(
        combine_body,
        out_shape=jax.ShapeDtypeStruct((n_tok, width), BF16),
        name="combine",
        compiler_params=limit(8),
    )(held(back.reshape(shape)), held(high), held(low))


def solution(mesh):
    in_specs = (
        P("aa", ("ba", "col")),
        P("aa", None),
        P("aa", None),
        P("aa", None, ("ba", "col")),
        P("aa", None, ("ba", "col")),
        P("aa", ("ba", "col"), None),
    )
    out_specs = P("aa", ("ba", "col"))
    return jax.shard_map(shards, mesh=mesh, in_specs=in_specs, out_specs=out_specs, check_vma=False)
```

time: 151 us -> 135 us (0.89)
  blocking collectives: 63.1 us -> 116 us
  waiting for transfers between devices: 49.3 us -> 3.05 us
  Pallas kernels: 25.5 us -> 10.6 us
  starting transfers between devices: 10.1 us -> 2.76 us
    all_to_all x0 -> x1, blocking collectives: none -> 53.1 us  [shards(): lax.all_to_all(pair.reshape(n_aa * n_col, CAP, width), axes, 0, 0, tiled=...]
    all_to_all x1 -> x0, waiting for transfers between devices: 45.7 us -> none  [shards(): lax.all_to_all(pair.reshape(n_aa * n_col, CAP, width), axes, 0, 0, tiled=...]
    pallas_call x5, Pallas kernels: 22.5 us -> 9.25 us  [the longest x1 4.33 us: shards(): pl.pallas_call(first_body, name='first', in_specs=[smem, vmem] + [hbm] *...]
    all_to_all x1 -> x0, starting transfers between devices: 6.2 us -> none  [shards(): lax.all_to_all(pair.reshape(n_aa * n_col, CAP, width), axes, 0, 0, tiled=...]
    pallas_call x1, Pallas kernels: 2.93 us -> 1.35 us  [shards(): pl.pallas_call(combine_body, out_shape=jax.ShapeDtypeStruct((n_tok, width...]
  transfers between devices with their start and end apart: 3 -> 2, of which waited for: 2 -> 1; matrix products, arithmetic and copies ran while one was open for 0% -> 0% of each run, Pallas kernels for 4% -> 4%
where the time goes in v2:
time: 135 us
  blocking collectives  116 us (86%)
  Pallas kernels  10.6 us (8%)
  waiting for transfers between devices  3.05 us (2%)
  starting transfers between devices  2.76 us (2%)
  local copies, waits for them, and re-layouts  2.41 us (2%)
    all_to_all x1, blocking collectives, shards(): lax.all_to_all(picked.reshape(n_aa * n_col, CAP, width), axes, 0, 0, tile...  62.9 us
    all_to_all x1, blocking collectives, shards(): lax.all_to_all(pair.reshape(n_aa * n_col, CAP, width), axes, 0, 0, tiled=...  53.1 us
    pallas_call x1, Pallas kernels, shards(): pl.pallas_call(first_body, name='first', in_specs=[smem, vmem] + [hbm] *...  4.33 us
    pallas_call x1, Pallas kernels, shards(): pl.pallas_call(second_body, name='second', in_specs=[smem] + [vmem] * 6,...  3.41 us
    ppermute x1, waiting for transfers between devices, shards(): got = lax.ppermute(sent, 'ba', swap)  3.05 us
  transfers between devices with their start and end apart: 2, of which 1 were waited for; matrix products, arithmetic and copies ran while one was open for 0% of the time, Pallas kernels for 4%

profile of v2, /device:TPU:1, one launch (start us, length us, event | category | flops | bytes accessed | tf_op | source)
XLA Modules:
  0.0 134.9 jit_solution(14375524755416963779)
XLA Ops:
  0.0 0.0 copy-start
  0.0 1.0 copy-done
  1.0 0.0 copy-start.1
  1.0 0.7 copy-done.1
  1.7 0.0 copy-start.2
  1.7 0.7 copy-done.2
  2.4 0.5 prepare.1
  2.9 62.9 %all_to_all.10 = bf16[128,8,896]{2,1,0:T(8,128)(2,1)S(1)} all-to-all(bf16[128,8,896]{2,1,0:T(8,128)(2,1)S(1)} %bitcast.14), channel_id=1, replica_groups=mesh['aa'=32,'ba'=2,'col'=4] {'aa','col'}, dimensions={0} | all-to-all | bytes 3670016 | tf_op jit(solution)/shard_map/all_to_all | solution.py:172
  65.9 2.7 %collective-permute-start = (bf16[32,4,8,896]{3,2,1,0:T(8,128)(2,1)S(1)}, bf16[32,4,8,896]{3,2,1,0:T(8,128)(2,1)}, u32[]{:S(2)}, u32[]{:S(2)}) collective-permute-start(bf16[32,4,8,896]{3,2,1,0:T(8,128)(2,1)S(1)} %bitcast.10), channel_id=1, source_target_pairs={{0,4},{4,0},{1,5},{5,1},{2,6},{6,2},{3,7},{7,3},{8,12},{12,8},{9,1... | collective-permute-start | bytes 5505032 | tf_op jit(solution)/shard_map/ppermute | solution.py:174
  68.5 4.3 %first.1 = (f32[256,256]{1,0:T(8,128)S(1)}, f32[256,256]{1,0:T(8,128)S(1)}, bf16[4,896,256]{2,1,0:T(8,128)(2,1)S(1)}, bf16[4,896,256]{2,1,0:T(8,128)(2,1)S(1)}, bf16[256,7168]{1,0:T(8,128)(2,1)S(1)}) custom-call(s32[1]{0:T(128)} %bitcast.b_ref, bf16[32,4,8,896]{3,2,1,0:T(8,128)(2,1)S(1)} %bitcast.11, bf16[8,896,256]{2,1,0:T(8,128)(2,1)} %bitcast.17, ...), custom_call_target="tpu_custom_call" | custom-call | tf_op jit(solution)/shard_map/first/pallas_call | solution.py:177
  72.9 0.0 collective-permute-done.x_ref
  72.9 3.4 %second.1 = (bf16[256,256]{1,0:T(8,128)(2,1)S(1)}, bf16[32,4,8,896]{3,2,1,0:T(8,128)(2,1)S(1)}) custom-call(s32[1]{0:T(128)} %bitcast.b_ref, bf16[32,4,8,896]{3,2,1,0:T(8,128)(2,1)} %collective-permute-done.x_ref, bf16[4,896,256]{2,1,0:T(8,128)(2,1)S(1)} %get-tuple-element.16.wg_ref, bf16[4,896,256]{2,1,0:T(8,128)(2,1)S(1)} %get-tuple-element.17.wu_ref, ...), custom_call_target="tpu_custom_call" | custom-call | tf_op jit(solution)/shard_map/second/pallas_call | solution.py:188
  76.3 0.1 collective-permute-start.1
  76.4 0.7 third.1.own_ref
  77.1 3.0 %collective-permute-done.1.other_ref = bf16[32,4,8,896]{3,2,1,0:T(8,128)(2,1)S(1)} collective-permute-done((bf16[32,4,8,896]{3,2,1,0:T(8,128)(2,1)S(1)}, bf16[32,4,8,896]{3,2,1,0:T(8,128)(2,1)S(1)}, u32[]{:S(2)}, u32[]{:S(2)}) %collective-permute-start.1) | collective-permute-done | bytes 1835040 | tf_op jit(solution)/shard_map/ppermute | solution.py:196
  80.2 0.3 pair.1
  80.5 53.1 %all_to_all.11 = bf16[128,8,896]{2,1,0:T(8,128)(2,1)S(1)} all-to-all(bf16[128,8,896]{2,1,0:T(8,128)(2,1)S(1)} %bitcast.12), channel_id=1, replica_groups=mesh['aa'=32,'ba'=2,'col'=4] {'aa','col'}, dimensions={0} | all-to-all | bytes 3670016 | tf_op jit(solution)/shard_map/all_to_all | solution.py:208
  133.6 1.4 %combine.1 = bf16[256,896]{1,0:T(8,128)(2,1)} custom-call(bf16[32,4,8,896]{3,2,1,0:T(8,128)(2,1)S(1)} %bitcast.13, bf16[256,256]{1,0:T(8,128)(2,1)S(1)} %get-tuple-element.23.high_ref, bf16[256,256]{1,0:T(8,128)(2,1)S(1)} %get-tuple-element.24.low_ref), custom_call_target="tpu_custom_call" | custom-call | tf_op jit(solution)/shard_map/combine/pallas_call | solution.py:209
Async XLA Ops:
  0.0 1.0 copy-start
  1.0 0.7 copy-start.1
  1.7 0.7 copy-start.2
  65.9 7.0 %collective-permute-start = (bf16[32,4,8,896]{3,2,1,0:T(8,128)(2,1)S(1)}, bf16[32,4,8,896]{3,2,1,0:T(8,128)(2,1)}, u32[]{:S(2)}, u32[]{:S(2)}) collective-permute-start(bf16[32,4,8,896]{3,2,1,0:T(8,128)(2,1)S(1)} %bitcast.10), channel_id=1, source_target_pairs={{0,4},{4,0},{1,5},{5,1},{2,6},{6,2},{3,7},{7,3},{8,12},{12,8},{9,1... | collective-permute-start | bytes 5505032 | tf_op jit(solution)/shard_map/ppermute | solution.py:174
  76.3 3.9 %collective-permute-start.1 = (bf16[32,4,8,896]{3,2,1,0:T(8,128)(2,1)S(1)}, bf16[32,4,8,896]{3,2,1,0:T(8,128)(2,1)S(1)}, u32[]{:S(2)}, u32[]{:S(2)}) collective-permute-start(bf16[32,4,8,896]{3,2,1,0:T(8,128)(2,1)S(1)} %get-tuple-element.22), channel_id=1, source_target_pairs={{0,4},{4,0},{1,5},{5,1},{2,6},{6,2},{3,7},{7,3},{8,12},{12,8},{9,1... | collective-permute-start | bytes 5505032 | tf_op jit(solution)/shard_map/ppermute | solution.py:196

commit v3 on v2

--- a/solution.py
+++ b/solution.py
@@ -12,6 +12,10 @@
 
 def held(x):
     return pltpu.with_memory_space_constraint(x, pltpu.VMEM)
+
+
+def far(x):
+    return pltpu.with_memory_space_constraint(x, pltpu.HBM)
 
 
 def limit(mib):
@@ -45,15 +49,21 @@
     return jnp.where(spread == slot, filled, 0.0).reshape(experts * CAP, tokens)
 
 
-def prepare_body(ids_ref, rw_ref, tok_ref, out_ref, high_ref, low_ref):
+def prepare_body(ids_hbm, rw_hbm, tok_hbm, out_ref, high_ref, low_ref, ids_ref, rw_ref, tok_ref, sems):
     experts, copies, cap, width = out_ref.shape
+    moves = [
+        pltpu.make_async_copy(ids_hbm, ids_ref, sems.at[0]),
+        pltpu.make_async_copy(rw_hbm, rw_ref, sems.at[1]),
+        pltpu.make_async_copy(tok_hbm, tok_ref, sems.at[2]),
+    ]
+    for move in moves:
+        move.start()
+    moves[0].wait()
+    moves[1].wait()
     ids = ids_ref[...]
     rw = rw_ref[...]
     pool, rank = slots_of(ids, experts)
     chooser = placed_of(rank, jnp.ones(rank.shape, F32)).astype(BF16)
-    rows = mm(chooser, tok_ref[...]).astype(BF16).reshape(experts, cap, width)
-    for j in range(copies):
-        out_ref[:, j] = rows
     share = jnp.zeros(pool.shape, F32)
     for k in range(ids.shape[0]):
         share = share + jnp.where(ids[k : k + 1, :] == pool, rw[k : k + 1, :], 0.0)
@@ -61,6 +71,10 @@
     high = weight.astype(BF16)
     high_ref[...] = high
     low_ref[...] = (weight - high.astype(F32)).astype(BF16)
+    moves[2].wait()
+    rows = mm(chooser, tok_ref[...]).astype(BF16).reshape(experts, cap, width)
+    for j in range(copies):
+        out_ref[:, j] = rows
 
 
 def gate_up(x_ref, wg_ref, wu_ref, ready):
@@ -76,7 +90,7 @@
     return g, u
 
 
-def first_body(b_ref, x_ref, wg_hbm, wu_hbm, wd_hbm, g_ref, u_ref, wg_ref, wu_ref, wd_ref, wg0_ref, wu0_ref, sems, late):
+def first_body(b_ref, x_ref, wg_hbm, wu_hbm, g_ref, u_ref, wg_ref, wu_ref, wg0_ref, wu0_ref, sems, late):
     b = b_ref[0]
     copies = x_ref.shape[1]
     near = [
@@ -86,15 +100,14 @@
         )
         for j in range(copies)
     ]
-    far = [
+    rest = [
         pltpu.make_async_copy(wg_hbm.at[pl.ds((1 - b) * copies, copies)], wg_ref, late.at[0]),
         pltpu.make_async_copy(wu_hbm.at[pl.ds((1 - b) * copies, copies)], wu_ref, late.at[1]),
-        pltpu.make_async_copy(wd_hbm, wd_ref, late.at[2]),
     ]
     for pair in near:
         for move in pair:
             move.start()
-    for move in far:
+    for move in rest:
         move.start()
 
     def ready(j):
@@ -102,7 +115,7 @@
             move.wait()
 
     g_ref[...], u_ref[...] = gate_up(x_ref, wg0_ref, wu0_ref, ready)
-    for move in far:
+    for move in rest:
         move.wait()
 
 
@@ -111,13 +124,19 @@
     return mm(h, wd_ref[:, pl.ds(at, width)])
 
 
-def second_body(b_ref, x_ref, wg_ref, wu_ref, g_ref, u_ref, wd_ref, h_ref, out_ref):
+def second_body(b_ref, x_hbm, wg_ref, wu_ref, g_ref, u_ref, wd_hbm, h_ref, out_ref, wd_ref, x_ref, sems):
     experts, copies, cap, width = x_ref.shape
-    g, u = gate_up(x_ref, wg_ref, wu_ref, lambda j: None)
+    rows = [pltpu.make_async_copy(x_hbm.at[:, j], x_ref.at[:, j], sems.at[j]) for j in range(copies)]
+    late = pltpu.make_async_copy(wd_hbm, wd_ref, sems.at[copies])
+    for move in rows:
+        move.start()
+    late.start()
+    g, u = gate_up(x_ref, wg_ref, wu_ref, lambda j: rows[j].wait())
     g = g + g_ref[...]
     u = u + u_ref[...]
     h = (g / (1.0 + jnp.exp(-g)) * u).astype(BF16)
     h_ref[...] = h
+    late.wait()
     for j in range(copies):
         out_ref[:, j] = down(1 - b_ref[0], j, h, wd_ref, copies, width).astype(BF16).reshape(experts, cap, width)
 
@@ -164,34 +183,41 @@
     picked, high, low = pl.pallas_call(
         prepare_body,
         name="prepare",
-        in_specs=[vmem] * 3,
+        in_specs=[hbm] * 3,
         out_shape=[pltpu.VMEM(shape, BF16), flat, flat],
         out_specs=[vmem] * 3,
+        scratch_shapes=[
+            pltpu.VMEM(ids.shape, jnp.int32),
+            pltpu.VMEM(rw.shape, F32),
+            pltpu.VMEM(tokens.shape, BF16),
+            pltpu.SemaphoreType.DMA((3,)),
+        ],
         compiler_params=limit(8),
-    )(ids, rw, tokens)
+    )(far(ids), far(rw), far(tokens))
     mine = lax.all_to_all(picked.reshape(n_aa * n_col, CAP, width), axes, 0, 0, tiled=True)
     mine = mine.reshape(shape)
     theirs = lax.ppermute(mine, "ba", swap)
 
     part = pltpu.VMEM((n_col, width, hid), BF16)
-    g, u, wg, wu, wd = pl.pallas_call(
+    g, u, wg, wu = pl.pallas_call(
         first_body,
         name="first",
-        in_specs=[smem, vmem] + [hbm] * 3,
-        out_shape=[acc, acc, part, part, pltpu.VMEM(params[2].shape, BF16)],
-        out_specs=[vmem] * 5,
-        scratch_shapes=[part, part, pltpu.SemaphoreType.DMA((2 * n_col,)), pltpu.SemaphoreType.DMA((3,))],
+        in_specs=[smem, vmem] + [hbm] * 2,
+        out_shape=[acc, acc, part, part],
+        out_specs=[vmem] * 4,
+        scratch_shapes=[part, part, pltpu.SemaphoreType.DMA((2 * n_col,)), pltpu.SemaphoreType.DMA((2,))],
         compiler_params=limit(16),
-    )(b, held(mine), *[pltpu.with_memory_space_constraint(p, pltpu.HBM) for p in params])
-    wg, wu, wd = held(wg), held(wu), held(wd)
-
-    hidden, sent = pl.pallas_call(
+    )(b, held(mine), far(params[0]), far(params[1]))
+
+    hidden, sent, wd = pl.pallas_call(
         second_body,
         name="second",
-        in_specs=[smem] + [vmem] * 6,
-        out_shape=[pltpu.VMEM((n_slot, hid), BF16), pltpu.VMEM(shape, BF16)],
-        compiler_params=limit(8),
-    )(b, held(theirs), wg, wu, held(g), held(u), wd)
+        in_specs=[smem, hbm] + [vmem] * 4 + [hbm],
+        out_shape=[pltpu.VMEM((n_slot, hid), BF16), pltpu.VMEM(shape, BF16), pltpu.VMEM(params[2].shape, BF16)],
+        out_specs=[vmem] * 3,
+        scratch_shapes=[pltpu.VMEM(shape, BF16), pltpu.SemaphoreType.DMA((n_col + 1,))],
+        compiler_params=limit(12),
+    )(b, far(theirs), held(wg), held(wu), held(g), held(u), far(params[2]))
 
     got = lax.ppermute(sent, "ba", swap)
     own = pl.pallas_call(
@@ -200,7 +226,7 @@
         in_specs=[smem] + [vmem] * 2,
         out_shape=pltpu.VMEM(shape, F32),
         compiler_params=limit(8),
-    )(b, held(hidden), wd)
+    )(b, held(hidden), held(wd))
     pair = pl.pallas_call(
         pair_body, name="pair", out_shape=pltpu.VMEM(shape, BF16), compiler_params=limit(8)
     )(held(own), held(got))

time: 135 us -> 133 us (0.985)
  local copies, waits for them, and re-layouts: 2.41 us -> 0 us
    unnamed x6 -> x0, local copies, waits for them, and re-layouts: 2.41 us -> none
  transfers between devices with their start and end apart: 2 -> 2, of which waited for: 1 -> 2; matrix products, arithmetic and copies ran while one was open for 0% -> 0% of each run, Pallas kernels for 4% -> 3%
where the time goes in v3:
time: 133 us
  blocking collectives  116 us (87%)
  Pallas kernels  10.5 us (8%)
  starting transfers between devices  3.12 us (2%)
  waiting for transfers between devices  2.97 us (2%)
    all_to_all x1, blocking collectives, shards(): lax.all_to_all(picked.reshape(n_aa * n_col, CAP, width), axes, 0, 0, tile...  62.9 us
    all_to_all x1, blocking collectives, shards(): lax.all_to_all(pair.reshape(n_aa * n_col, CAP, width), axes, 0, 0, tiled=...  53 us
    pallas_call x1, Pallas kernels, shards(): pl.pallas_call(second_body, name='second', in_specs=[smem, hbm] + [vmem]...  3.38 us
    pallas_call x1, Pallas kernels, shards(): pl.pallas_call(first_body, name='first', in_specs=[smem, vmem] + [hbm] *...  3.26 us
    ppermute x1, waiting for transfers between devices, shards(): got = lax.ppermute(sent, 'ba', swap)  2.69 us
  transfers between devices with their start and end apart: 2, of which 2 were waited for; matrix products, arithmetic and copies ran while one was open for 0% of the time, Pallas kernels for 3%

profile of v3, /device:TPU:1, one launch (start us, length us, event | category | flops | bytes accessed | tf_op | source)
XLA Modules:
  0.0 132.5 jit_solution(4320987272477139816)
XLA Ops:
  0.0 1.4 %prepare.1 = (bf16[32,4,8,896]{3,2,1,0:T(8,128)(2,1)S(1)}, bf16[256,256]{1,0:T(8,128)(2,1)S(1)}, bf16[256,256]{1,0:T(8,128)(2,1)S(1)}) custom-call(s32[8,256]{1,0:T(8,128)} %bitcast.18, f32[8,256]{1,0:T(8,128)} %bitcast.19, bf16[256,896]{1,0:T(8,128)(2,1)} %tok_hbm.1), custom_call_target="tpu_custom_call" | custom-call | tf_op jit(solution)/shard_map/prepare/pallas_call | solution.py:183
  1.4 62.9 %all_to_all.10 = bf16[128,8,896]{2,1,0:T(8,128)(2,1)S(1)} all-to-all(bf16[128,8,896]{2,1,0:T(8,128)(2,1)S(1)} %bitcast.14), channel_id=1, replica_groups=mesh['aa'=32,'ba'=2,'col'=4] {'aa','col'}, dimensions={0} | all-to-all | bytes 3670016 | tf_op jit(solution)/shard_map/all_to_all | solution.py:197
  64.4 2.7 %collective-permute-start = (bf16[32,4,8,896]{3,2,1,0:T(8,128)(2,1)S(1)}, bf16[32,4,8,896]{3,2,1,0:T(8,128)(2,1)}, u32[]{:S(2)}, u32[]{:S(2)}) collective-permute-start(bf16[32,4,8,896]{3,2,1,0:T(8,128)(2,1)S(1)} %bitcast.10), channel_id=1, source_target_pairs={{0,4},{4,0},{1,5},{5,1},{2,6},{6,2},{3,7},{7,3},{8,12},{12,8},{9,1... | collective-permute-start | bytes 5505032 | tf_op jit(solution)/shard_map/ppermute | solution.py:199
  67.0 3.3 %first.1 = (f32[256,256]{1,0:T(8,128)S(1)}, f32[256,256]{1,0:T(8,128)S(1)}, bf16[4,896,256]{2,1,0:T(8,128)(2,1)S(1)}, bf16[4,896,256]{2,1,0:T(8,128)(2,1)S(1)}) custom-call(s32[1]{0:T(128)} %bitcast.b_ref, bf16[32,4,8,896]{3,2,1,0:T(8,128)(2,1)S(1)} %bitcast.11, bf16[8,896,256]{2,1,0:T(8,128)(2,1)} %bitcast.15, bf16[8,896,256]{2,1,0:T(8,128)(2,1)} %bitcast.16), custom_call_target="tpu_custom_call" | custom-call | tf_op jit(solution)/shard_map/first/pallas_call | solution.py:202
  70.3 0.3 collective-permute-done.x_hbm
  70.6 3.4 %second.1 = (bf16[256,256]{1,0:T(8,128)(2,1)S(1)}, bf16[32,4,8,896]{3,2,1,0:T(8,128)(2,1)S(1)}, bf16[256,7168]{1,0:T(8,128)(2,1)S(1)}) custom-call(s32[1]{0:T(128)} %bitcast.b_ref, bf16[32,4,8,896]{3,2,1,0:T(8,128)(2,1)} %collective-permute-done.x_hbm, bf16[4,896,256]{2,1,0:T(8,128)(2,1)S(1)} %get-tuple-element.16.wg_ref, ...), custom_call_target="tpu_custom_call" | custom-call | tf_op jit(solution)/shard_map/second/pallas_call | solution.py:212
  73.9 0.5 collective-permute-start.1
  74.4 0.7 third.1.own_ref
  75.1 2.7 %collective-permute-done.1.other_ref = bf16[32,4,8,896]{3,2,1,0:T(8,128)(2,1)S(1)} collective-permute-done((bf16[32,4,8,896]{3,2,1,0:T(8,128)(2,1)S(1)}, bf16[32,4,8,896]{3,2,1,0:T(8,128)(2,1)S(1)}, u32[]{:S(2)}, u32[]{:S(2)}) %collective-permute-start.1) | collective-permute-done | bytes 1835040 | tf_op jit(solution)/shard_map/ppermute | solution.py:222
  77.8 0.4 pair.1
  78.2 53.0 %all_to_all.11 = bf16[128,8,896]{2,1,0:T(8,128)(2,1)S(1)} all-to-all(bf16[128,8,896]{2,1,0:T(8,128)(2,1)S(1)} %bitcast.12), channel_id=1, replica_groups=mesh['aa'=32,'ba'=2,'col'=4] {'aa','col'}, dimensions={0} | all-to-all | bytes 3670016 | tf_op jit(solution)/shard_map/all_to_all | solution.py:234
  131.2 1.4 %combine.1 = bf16[256,896]{1,0:T(8,128)(2,1)} custom-call(bf16[32,4,8,896]{3,2,1,0:T(8,128)(2,1)S(1)} %bitcast.13, bf16[256,256]{1,0:T(8,128)(2,1)S(1)} %get-tuple-element.23.high_ref, bf16[256,256]{1,0:T(8,128)(2,1)S(1)} %get-tuple-element.24.low_ref), custom_call_target="tpu_custom_call" | custom-call | tf_op jit(solution)/shard_map/combine/pallas_call | solution.py:235
Async XLA Ops:
  64.4 6.2 %collective-permute-start = (bf16[32,4,8,896]{3,2,1,0:T(8,128)(2,1)S(1)}, bf16[32,4,8,896]{3,2,1,0:T(8,128)(2,1)}, u32[]{:S(2)}, u32[]{:S(2)}) collective-permute-start(bf16[32,4,8,896]{3,2,1,0:T(8,128)(2,1)S(1)} %bitcast.10), channel_id=1, source_target_pairs={{0,4},{4,0},{1,5},{5,1},{2,6},{6,2},{3,7},{7,3},{8,12},{12,8},{9,1... | collective-permute-start | bytes 5505032 | tf_op jit(solution)/shard_map/ppermute | solution.py:199
  73.9 3.9 %collective-permute-start.1 = (bf16[32,4,8,896]{3,2,1,0:T(8,128)(2,1)S(1)}, bf16[32,4,8,896]{3,2,1,0:T(8,128)(2,1)S(1)}, u32[]{:S(2)}, u32[]{:S(2)}) collective-permute-start(bf16[32,4,8,896]{3,2,1,0:T(8,128)(2,1)S(1)} %get-tuple-element.22), channel_id=1, source_target_pairs={{0,4},{4,0},{1,5},{5,1},{2,6},{6,2},{3,7},{7,3},{8,12},{12,8},{9,1... | collective-permute-start | bytes 5505032 | tf_op jit(solution)/shard_map/ppermute | solution.py:222

commit v4 on v3

v4 whole, which is shorter than its diff:
```python
import jax
import jax.numpy as jnp
from jax import lax
from jax.experimental import pallas as pl
from jax.experimental.pallas import tpu as pltpu
from jax.sharding import PartitionSpec as P

CAP = 8
F32 = jnp.float32
BF16 = jnp.bfloat16


def held(x):
    return pltpu.with_memory_space_constraint(x, pltpu.VMEM)


def far(x):
    return pltpu.with_memory_space_constraint(x, pltpu.HBM)


def limit(mib):
    return pltpu.CompilerParams(vmem_limit_bytes=mib * 2**20)


def mm(a, b):
    return jnp.dot(a, b, preferred_element_type=F32)


def slots_of(ids, experts):
    top, tokens = ids.shape
    pool = lax.broadcasted_iota(jnp.int32, (experts, tokens), 0)
    hit = jnp.zeros((experts, tokens), F32)
    for k in range(top):
        hit = hit + jnp.where(ids[k : k + 1, :] == pool, 1.0, 0.0)
    earlier = lax.broadcasted_iota(jnp.int32, (tokens, tokens), 0)
    later = lax.broadcasted_iota(jnp.int32, (tokens, tokens), 1)
    before = mm(hit.astype(BF16), jnp.where(earlier < later, 1.0, 0.0).astype(BF16))
    rank = before.astype(jnp.int32)
    kept = (hit > 0.0) & (rank < CAP)
    rank = jnp.where(kept, rank, -1)
    return pool, rank


def placed_of(rank, value):
    experts, tokens = rank.shape
    slot = lax.broadcasted_iota(jnp.int32, (experts, CAP, tokens), 1)
    spread = lax.broadcast_in_dim(rank, (experts, CAP, tokens), (0, 2))
    filled = lax.broadcast_in_dim(value, (experts, CAP, tokens), (0, 2))
    return jnp.where(spread == slot, filled, 0.0).reshape(experts * CAP, tokens)


def prepare_body(ids_hbm, rw_hbm, tok_hbm, out_hbm, high_ref, low_ref, ids_ref, rw_ref, tok_ref, rows_ref, sems, sent):
    experts, copies, cap, width = out_hbm.shape
    moves = [
        pltpu.make_async_copy(ids_hbm, ids_ref, sems.at[0]),
        pltpu.make_async_copy(rw_hbm, rw_ref, sems.at[1]),
        pltpu.make_async_copy(tok_hbm, tok_ref, sems.at[2]),
    ]
    for move in moves:
        move.start()
    moves[0].wait()
    ids = ids_ref[...]
    pool, rank = slots_of(ids, experts)
    chooser = placed_of(rank, jnp.ones(rank.shape, F32)).astype(BF16)
    moves[2].wait()
    rows_ref[...] = mm(chooser, tok_ref[...]).astype(BF16).reshape(experts, cap, width)
    out = [pltpu.make_async_copy(rows_ref, out_hbm.at[:, j], sent.at[j]) for j in range(copies)]
    for move in out:
        move.start()
    moves[1].wait()
    rw = rw_ref[...]
    share = jnp.zeros(pool.shape, F32)
    for k in range(ids.shape[0]):
        share = share + jnp.where(ids[k : k + 1, :] == pool, rw[k : k + 1, :], 0.0)
    weight = placed_of(rank, share).T
    high = weight.astype(BF16)
    high_ref[...] = high
    low_ref[...] = (weight - high.astype(F32)).astype(BF16)
    for move in out:
        move.wait()


def gate_up(b_ref, x_ref, wg_hbm, wu_hbm, wg_ref, wu_ref, sems):
    copies, width = x_ref.shape[1], x_ref.shape[3]
    at = b_ref[0] * copies
    moves = [
        (
            pltpu.make_async_copy(wg_hbm.at[at + j], wg_ref.at[j], sems.at[j]),
            pltpu.make_async_copy(wu_hbm.at[at + j], wu_ref.at[j], sems.at[copies + j]),
        )
        for j in range(copies)
    ]
    for pair in moves:
        for move in pair:
            move.start()
    g = u = None
    for j in range(copies):
        x = x_ref[:, j].reshape(-1, width)
        moves[j][0].wait()
        dg = mm(x, wg_ref[j])
        moves[j][1].wait()
        du = mm(x, wu_ref[j])
        g = dg if g is None else g + dg
        u = du if u is None else u + du
    return g, u


def sums_body(b_ref, x_ref, wg_hbm, wu_hbm, out_ref, wg_ref, wu_ref, sems):
    out_ref[0], out_ref[1] = gate_up(b_ref, x_ref, wg_hbm, wu_hbm, wg_ref, wu_ref, sems)


def hidden_body(own_ref, other_ref, out_ref):
    g = own_ref[0] + other_ref[0]
    u = own_ref[1] + other_ref[1]
    out_ref[...] = (g / (1.0 + jnp.exp(-g)) * u).astype(BF16)


def near_body(b_ref, h_ref, mine_hbm, theirs_hbm, out_ref, late_ref, w_ref, sems):
    experts, copies, cap, width = out_ref.shape
    moves = []
    for n, (hbm, ref) in enumerate(((mine_hbm, w_ref), (theirs_hbm, late_ref))):
        for j in range(copies):
            at = pl.multiple_of((b_ref[0] * copies + j) * width, 128)
            moves.append(pltpu.make_async_copy(hbm.at[:, pl.ds(at, width)], ref.at[j], sems.at[n * copies + j]))
    for move in moves:
        move.start()
    h = h_ref[...]
    for j in range(copies):
        moves[j].wait()
        out_ref[:, j] = mm(h, w_ref[j]).reshape(experts, cap, width)
    for j in range(copies):
        moves[copies + j].wait()


def far_body(h_ref, w_ref, own_ref, out_ref):
    experts, copies, cap, width = out_ref.shape
    h = h_ref[...]
    for j in range(copies):
        other = mm(h, w_ref[j]).reshape(experts, cap, width)
        out_ref[:, j] = (own_ref[:, j] + other).astype(BF16)


def combine_body(r_ref, high_ref, low_ref, out_ref):
    experts, copies, cap, width = r_ref.shape
    total = r_ref[:, 0].astype(F32)
    for j in range(1, copies):
        total = total + r_ref[:, j].astype(F32)
    rows = total.astype(BF16).reshape(experts * cap, width)
    out_ref[...] = (mm(high_ref[...], rows) + mm(low_ref[...], rows)).astype(BF16)


def shards(tokens, expert_ids, route_weight, w_gate, w_up, w_down):
    n_aa, n_ba, n_col = lax.axis_size("aa"), lax.axis_size("ba"), lax.axis_size("col")
    n_tok, width = tokens.shape
    hid = w_gate.shape[2]
    n_slot = n_aa * CAP
    ids = expert_ids.T
    rw = route_weight.T
    b = lax.axis_index("ba").astype(jnp.int32).reshape(1)
    params = [w_gate.reshape(n_ba * n_col, width, hid), w_up.reshape(n_ba * n_col, width, hid), w_down[0]]
    swap = [(i, n_ba - 1 - i) for i in range(n_ba)]
    axes = ("aa", "col")
    swapped = [lax.ppermute(p, "ba", swap) for p in params]
    shape = (n_aa, n_col, CAP, width)
    smem = pl.BlockSpec(memory_space=pltpu.SMEM)
    vmem = pl.BlockSpec(memory_space=pltpu.VMEM)

    hbm = pl.BlockSpec(memory_space=pl.ANY)
    flat = pltpu.VMEM((n_tok, n_slot), BF16)
    picked, high, low = pl.pallas_call(
        prepare_body,
        name="prepare",
        in_specs=[hbm] * 3,
        out_shape=[pltpu.HBM(shape, BF16), flat, flat],
        out_specs=[hbm, vmem, vmem],
        scratch_shapes=[
            pltpu.VMEM(ids.shape, jnp.int32),
            pltpu.VMEM(rw.shape, F32),
            pltpu.VMEM(tokens.shape, BF16),
            pltpu.VMEM((n_aa, CAP, width), BF16),
            pltpu.SemaphoreType.DMA((3,)),
            pltpu.SemaphoreType.DMA((n_col,)),
        ],
        compiler_params=limit(8),
    )(far(ids), far(rw), far(tokens))
    mine = lax.all_to_all(picked.reshape(n_aa * n_col, CAP, width), axes, 0, 0, tiled=True)
    mine = mine.reshape(shape)

    part = pltpu.VMEM((n_col, width, hid), BF16)
    sums = lambda name, gate, up: pl.pallas_call(
        sums_body,
        name=name,
        in_specs=[smem, vmem, hbm, hbm],
        out_shape=pltpu.VMEM((2, n_slot, hid), F32),
        out_specs=vmem,
        scratch_shapes=[part, part, pltpu.SemaphoreType.DMA((2 * n_col,))],
        compiler_params=limit(12),
    )(b, held(mine), far(gate), far(up))
    sent = sums("cross", swapped[0], swapped[1])
    got = lax.ppermute(sent, "ba", swap)
    own = sums("own", params[0], params[1])
    hidden = pl.pallas_call(
        hidden_body, name="hidden", out_shape=pltpu.VMEM((n_slot, hid), BF16), compiler_params=limit(8)
    )(held(own), held(got))
    other = lax.ppermute(hidden, "ba", swap)

    half = pltpu.VMEM((n_col, hid, width), BF16)
    near, late = pl.pallas_call(
        near_body,
        name="near",
        in_specs=[smem, vmem, hbm, hbm],
        out_shape=[pltpu.VMEM(shape, F32), half],
        out_specs=[vmem] * 2,
        scratch_shapes=[half, pltpu.SemaphoreType.DMA((2 * n_col,))],
        compiler_params=limit(12),
    )(b, held(hidden), far(params[2]), far(swapped[2]))
    pair = pl.pallas_call(
        far_body, name="far", out_shape=pltpu.VMEM(shape, BF16), compiler_params=limit(8)
    )(held(other), held(late), held(near))

    back = lax.all_to_all(pair.reshape(n_aa * n_col, CAP, width), axes, 0, 0, tiled=True)
    return pl.pallas_call(
        combine_body,
        out_shape=jax.ShapeDtypeStruct((n_tok, width), BF16),
        name="combine",
        compiler_params=limit(8),
    )(held(back.reshape(shape)), held(high), held(low))


def solution(mesh):
    in_specs = (
        P("aa", ("ba", "col")),
        P("aa", None),
        P("aa", None),
        P("aa", None, ("ba", "col")),
        P("aa", None, ("ba", "col")),
        P("aa", ("ba", "col"), None),
    )
    out_specs = P("aa", ("ba", "col"))
    return jax.shard_map(shards, mesh=mesh, in_specs=in_specs, out_specs=out_specs, check_vma=False)
```

time: 133 us -> 135 us (1.015)
  blocking collectives: 116 us -> 53 us
  waiting for transfers between devices: 2.97 us -> 46.1 us
  starting transfers between devices: 3.12 us -> 20.6 us
  Pallas kernels: 10.5 us -> 14.7 us
    all_to_all x1 -> x0, blocking collectives: 62.9 us -> none  [shards(): lax.all_to_all(picked.reshape(n_aa * n_col, CAP, width), axes, 0, 0, tile...]
    all_to_all x0 -> x1, waiting for transfers between devices: none -> 46 us  [shards(): lax.all_to_all(picked.reshape(n_aa * n_col, CAP, width), axes, 0, 0, tile...]
    all_to_all x0 -> x1, starting transfers between devices: none -> 13.8 us  [shards(): lax.all_to_all(picked.reshape(n_aa * n_col, CAP, width), axes, 0, 0, tile...]
    pallas_call x4 -> x5, Pallas kernels: 7.73 us -> 10.7 us  [the longest x2 7.55 us: shards(): pl.pallas_call(sums_body, name=name, in_specs=[smem, vmem, hbm, hbm], out...]
    ppermute x1, waiting for transfers between devices: 2.69 us -> 0.01 us  [shards(): got = lax.ppermute(sent, 'ba', swap)]
    ppermute x1, starting transfers between devices: 0.46 us -> 2.65 us  [shards(): got = lax.ppermute(sent, 'ba', swap)]
    ppermute x1 -> x4, starting transfers between devices: 2.66 us -> 4.18 us  [the longest x3 4.08 us: shards(): swapped = [lax.ppermute(p, 'ba', swap) for p in params]]
  transfers between devices with their start and end apart: 2 -> 6, of which waited for: 2 -> 1; matrix products, arithmetic and copies ran while one was open for 0% -> 0% of each run, Pallas kernels for 3% -> 9%
where the time goes in v4:
time: 135 us
  blocking collectives  53 us (39%)
  waiting for transfers between devices  46.1 us (34%)
  starting transfers between devices  20.6 us (15%)
  Pallas kernels  14.7 us (11%)
    all_to_all x1, blocking collectives, shards(): lax.all_to_all(pair.reshape(n_aa * n_col, CAP, width), axes, 0, 0, tiled=...  53 us
    all_to_all x1, waiting for transfers between devices, shards(): lax.all_to_all(picked.reshape(n_aa * n_col, CAP, width), axes, 0, 0, tile...  46 us
    all_to_all x1, starting transfers between devices, shards(): lax.all_to_all(picked.reshape(n_aa * n_col, CAP, width), axes, 0, 0, tile...  13.8 us
    pallas_call x2, Pallas kernels, shards(): pl.pallas_call(sums_body, name=name, in_specs=[smem, vmem, hbm, hbm], out...  7.55 us
    ppermute x3, starting transfers between devices, shards(): swapped = [lax.ppermute(p, 'ba', swap) for p in params]  4.08 us
  transfers between devices with their start and end apart: 6, of which 1 were waited for; matrix products, arithmetic and copies ran while one was open for 0% of the time, Pallas kernels for 9%

profile of v4, /device:TPU:1, one launch (start us, length us, event | category | flops | bytes accessed | tf_op | source)
XLA Modules:
  0.0 134.5 jit_solution(4671527213719935708)
XLA Ops:
  0.0 3.2 %collective-permute-start = (bf16[8,896,256]{2,1,0:T(8,128)(2,1)}, bf16[8,896,256]{2,1,0:T(8,128)(2,1)}, u32[]{:S(2)}, u32[]{:S(2)}) collective-permute-start(bf16[8,896,256]{2,1,0:T(8,128)(2,1)} %bitcast.14), channel_id=1, source_target_pairs={{0,4},{4,0},{1,5},{5,1},{2,6},{6,2},{3,7},{7,3},{8,12},{12,8},{9,1... | collective-permute-start | bytes 11010056 | tf_op jit(solution)/shard_map/ppermute | solution.py:163
  3.2 0.0 collective-permute-start.1
  3.2 2.7 %prepare.1 = (bf16[32,4,8,896]{3,2,1,0:T(8,128)(2,1)}, bf16[256,256]{1,0:T(8,128)(2,1)S(1)}, bf16[256,256]{1,0:T(8,128)(2,1)S(1)}) custom-call(s32[8,256]{1,0:T(8,128)} %bitcast.21, f32[8,256]{1,0:T(8,128)} %bitcast.22, bf16[256,896]{1,0:T(8,128)(2,1)} %tok_hbm.1), custom_call_target="tpu_custom_call" | custom-call | tf_op jit(solution)/shard_map/prepare/pallas_call | solution.py:170
  5.9 13.8 %all-to-all-start = ((bf16[128,8,896]{2,1,0:T(8,128)(2,1)}), bf16[128,8,896]{2,1,0:T(8,128)(2,1)S(1)}, u32[]{:S(2)}, u32[]{:S(2)}) async-start(bf16[128,8,896]{2,1,0:T(8,128)(2,1)} %bitcast.20), calls=%async_computation | async-start | bytes 3670016 | tf_op jit(solution)/shard_map/all_to_all | solution.py:186
  19.7 0.9 collective-permute-start.4
  20.6 46.0 %all-to-all-done = bf16[128,8,896]{2,1,0:T(8,128)(2,1)S(1)} async-done(((bf16[128,8,896]{2,1,0:T(8,128)(2,1)}), bf16[128,8,896]{2,1,0:T(8,128)(2,1)S(1)}, u32[]{:S(2)}, u32[]{:S(2)}) %all-to-all-start) | async-done | bytes 1835040 | tf_op jit(solution)/shard_map/all_to_all | solution.py:186
  66.6 0.0 collective-permute-done.wg_hbm
  66.6 0.0 collective-permute-done.1.wu_hbm
  66.6 3.8 %cross.1 = f32[2,256,256]{2,1,0:T(8,128)S(1)} custom-call(s32[1]{0:T(128)} %bitcast.b_ref, bf16[32,4,8,896]{3,2,1,0:T(8,128)(2,1)S(1)} %bitcast.10, bf16[8,896,256]{2,1,0:T(8,128)(2,1)} %collective-permute-done.wg_hbm, bf16[8,896,256]{2,1,0:T(8,128)(2,1)} %collective-permute-done.1.wu_hbm), custom_call_target="tpu_custom_call" | custom-call | tf_op jit(solution)/shard_map/cross/pallas_call | solution.py:190
  70.4 2.7 %collective-permute-start.2 = (f32[2,256,256]{2,1,0:T(8,128)S(1)}, f32[2,256,256]{2,1,0:T(8,128)S(1)}, u32[]{:S(2)}, u32[]{:S(2)}) collective-permute-start(f32[2,256,256]{2,1,0:T(8,128)S(1)} %cross.1), channel_id=1, source_target_pairs={{0,4},{4,0},{1,5},{5,1},{2,6},{6,2},{3,7},{7,3},{8,12},{12,8},{9,1... | collective-permute-start | bytes 1572872 | tf_op jit(solution)/shard_map/ppermute | solution.py:200
  73.1 3.8 %own.1.own_ref = f32[2,256,256]{2,1,0:T(8,128)S(1)} custom-call(s32[1]{0:T(128)} %bitcast.b_ref, bf16[32,4,8,896]{3,2,1,0:T(8,128)(2,1)S(1)} %bitcast.11, bf16[8,896,256]{2,1,0:T(8,128)(2,1)} %bitcast.15, bf16[8,896,256]{2,1,0:T(8,128)(2,1)} %bitcast.17), custom_call_target="tpu_custom_call" | custom-call | tf_op jit(solution)/shard_map/own/pallas_call | solution.py:190
  76.9 0.0 collective-permute-done.2.other_ref
  76.9 0.1 hidden.1.h_ref
  77.0 0.1 collective-permute-start.3
  77.1 0.0 collective-permute-done.4.theirs_hbm
  77.1 2.3 %near.1 = (f32[32,4,8,896]{3,2,1,0:T(8,128)S(1)}, bf16[4,256,896]{2,1,0:T(8,128)(2,1)S(1)}) custom-call(s32[1]{0:T(128)} %bitcast.b_ref, bf16[256,256]{1,0:T(8,128)(2,1)S(1)} %hidden.1.h_ref, bf16[256,7168]{1,0:T(8,128)(2,1)} %bitcast.19, bf16[256,7168]{1,0:T(8,128)(2,1)} %collective-permute-done.4.theirs_hbm), custom_call_target="tpu_custom_call" | custom-call | tf_op jit(solution)/shard_map/near/pallas_call | solution.py:208
  79.4 0.0 collective-permute-done.3.h_ref
  79.4 0.7 far.1
  80.1 53.0 %all_to_all.10 = bf16[128,8,896]{2,1,0:T(8,128)(2,1)S(1)} all-to-all(bf16[128,8,896]{2,1,0:T(8,128)(2,1)S(1)} %bitcast.12), channel_id=1, replica_groups=mesh['aa'=32,'ba'=2,'col'=4] {'aa','col'}, dimensions={0} | all-to-all | bytes 3670016 | tf_op jit(solution)/shard_map/all_to_all | solution.py:221
  133.2 1.4 %combine.1 = bf16[256,896]{1,0:T(8,128)(2,1)} custom-call(bf16[32,4,8,896]{3,2,1,0:T(8,128)(2,1)S(1)} %bitcast.13, bf16[256,256]{1,0:T(8,128)(2,1)S(1)} %get-tuple-element.13.high_ref, bf16[256,256]{1,0:T(8,128)(2,1)S(1)} %get-tuple-element.14.low_ref), custom_call_target="tpu_custom_call" | custom-call | tf_op jit(solution)/shard_map/combine/pallas_call | solution.py:222
Async XLA Ops:
  0.0 66.6 %collective-permute-start = (bf16[8,896,256]{2,1,0:T(8,128)(2,1)}, bf16[8,896,256]{2,1,0:T(8,128)(2,1)}, u32[]{:S(2)}, u32[]{:S(2)}) collective-permute-start(bf16[8,896,256]{2,1,0:T(8,128)(2,1)} %bitcast.14), channel_id=1, source_target_pairs={{0,4},{4,0},{1,5},{5,1},{2,6},{6,2},{3,7},{7,3},{8,12},{12,8},{9,1... | collective-permute-start | bytes 11010056 | tf_op jit(solution)/shard_map/ppermute | solution.py:163
  3.2 63.4 %collective-permute-start.1 = (bf16[8,896,256]{2,1,0:T(8,128)(2,1)}, bf16[8,896,256]{2,1,0:T(8,128)(2,1)}, u32[]{:S(2)}, u32[]{:S(2)}) collective-permute-start(bf16[8,896,256]{2,1,0:T(8,128)(2,1)} %bitcast.16), channel_id=1, source_target_pairs={{0,4},{4,0},{1,5},{5,1},{2,6},{6,2},{3,7},{7,3},{8,12},{12,8},{9,1... | collective-permute-start | bytes 11010056 | tf_op jit(solution)/shard_map/ppermute | solution.py:163
  5.9 60.7 %all-to-all-start = ((bf16[128,8,896]{2,1,0:T(8,128)(2,1)}), bf16[128,8,896]{2,1,0:T(8,128)(2,1)S(1)}, u32[]{:S(2)}, u32[]{:S(2)}) async-start(bf16[128,8,896]{2,1,0:T(8,128)(2,1)} %bitcast.20), calls=%async_computation | async-start | bytes 3670016 | tf_op jit(solution)/shard_map/all_to_all | solution.py:186
  19.7 57.4 %collective-permute-start.4 = (bf16[256,7168]{1,0:T(8,128)(2,1)}, bf16[256,7168]{1,0:T(8,128)(2,1)}, u32[]{:S(2)}, u32[]{:S(2)}) collective-permute-start(bf16[256,7168]{1,0:T(8,128)(2,1)} %bitcast.18), channel_id=1, source_target_pairs={{0,4},{4,0},{1,5},{5,1},{2,6},{6,2},{3,7},{7,3},{8,12},{12,8},{9,1... | collective-permute-start | bytes 11010056 | tf_op jit(solution)/shard_map/ppermute | solution.py:163
  70.4 6.4 %collective-permute-start.2 = (f32[2,256,256]{2,1,0:T(8,128)S(1)}, f32[2,256,256]{2,1,0:T(8,128)S(1)}, u32[]{:S(2)}, u32[]{:S(2)}) collective-permute-start(f32[2,256,256]{2,1,0:T(8,128)S(1)} %cross.1), channel_id=1, source_target_pairs={{0,4},{4,0},{1,5},{5,1},{2,6},{6,2},{3,7},{7,3},{8,12},{12,8},{9,1... | collective-permute-start | bytes 1572872 | tf_op jit(solution)/shard_map/ppermute | solution.py:200
  77.0 2.4 %collective-permute-start.3 = (bf16[256,256]{1,0:T(8,128)(2,1)S(1)}, bf16[256,256]{1,0:T(8,128)(2,1)S(1)}, u32[]{:S(2)}, u32[]{:S(2)}) collective-permute-start(bf16[256,256]{1,0:T(8,128)(2,1)S(1)} %hidden.1.h_ref), channel_id=1, source_target_pairs={{0,4},{4,0},{1,5},{5,1},{2,6},{6,2},{3,7},{7,3},{8,12},{12,8},{9,1... | collective-permute-start | bytes 393224 | tf_op jit(solution)/shard_map/ppermute | solution.py:205
